TPU v7x, 32 devices: a whole 2x2x4 slice. The times are simulated.
32 devices in a mesh: parts: 2 (over x), shot: 2 (over core), space: 8 (over z, y).
Axes of the slice: x: 2, y: 2, z: 4, core: 2. Of those that a mesh axis runs over, the one named last changes fastest.
Arguments:
- image: float32 [3200, 2, 192], P(('parts', 'space')), parts along dimension 0, may hold values from -6 to 6
- coil_maps: bfloat16 [16, 3200, 2, 192], P(None, ('parts', 'space')), parts along dimension 1, may hold values from -1.5 to 1.5
- psf_phase: float32 [3200, 576], P(('parts', 'space')), parts along dimension 0, may hold values from -3.140625 to 3.140625
- line_mask: int32 [4, 200], P(('parts', 'shot')), parts along dimension 0, may hold values 0 or 1
- motion: int32 [4, 3], P(('parts', 'shot')), parts along dimension 0, may hold values from 0 to 16
Outputs:
- result: float32 [3200, 2, 192], P(('parts', 'space')), parts along dimension 0
There are 2 independent parts, one for each index of `parts`. A program takes and returns all parts, laid end to end along the dimension named above; each array names one. Nothing has to cross between parts.
Inputs may be any that keep to these rules, and one draw needn't show every extreme that they name: `motion`: column 0 selects the rotation angle, columns 1 and 2 the shifts along x and y.
All inputs are finite; a program needn't handle non-finite values. No bound on the sum of `line_mask` on one device may be relied on, other than what follows from the above.
Results may differ from a plain program's by a relative error of at most 0.003.
Values may be sent and summed in bfloat16 or wider, within the bound.
A program may use at most 64 MiB of HBM per device.

v0:
```python
import functools
import math

import jax
import jax.numpy as jnp
import numpy as np
from jax import lax
from jax.experimental import pallas as pl
from jax.experimental.pallas import tpu as pltpu
from jax.sharding import PartitionSpec as P

NY = 200
LEVELS = 17


PRECISE = lax.Precision.HIGHEST
ANGLE_STEP = 0.02
SHIFT_STEP = 0.5


def from_partner(value, axis, apart):
    mask = 2**apart
    pairs = [(source, source ^ mask) for source in range(lax.axis_size(axis))]
    return lax.ppermute(value, axis, pairs)


def dft_parts(size_in, size_out, modulus, sign):
    inputs = jnp.arange(size_in, dtype=jnp.int32)[:, None]
    outputs = jnp.arange(size_out, dtype=jnp.int32)[None, :]
    angle = (inputs * outputs % modulus).astype(jnp.float32) * (2.0 * jnp.pi / modulus)
    factor = float(modulus) ** (-0.5)
    return (jnp.cos(angle) * factor, jnp.sin(angle) * (sign * factor))


def block(parts):
    real_part, imag_part = parts
    upper = jnp.concatenate([real_part, imag_part], 1)
    bottom = jnp.concatenate([-imag_part, real_part], 1)
    return jnp.concatenate([upper, bottom], 0)


def quad(real_part, imag_part):
    return jnp.stack(
        [jnp.stack([real_part, -imag_part], 1), jnp.stack([imag_part, real_part], 1)], 0
    )


def signed_freq(length):
    counter = jnp.arange(length, dtype=jnp.int32)
    return jnp.where(counter < length // 2, counter, counter - length).astype(jnp.float32)


def turn_phase(values, phase):
    cosine = jnp.cos(phase)
    sine_part = jnp.sin(phase)
    real_part = values[..., 0, :]
    imag_part = values[..., 1, :]
    return jnp.stack(
        [real_part * cosine - imag_part * sine_part, real_part * sine_part + imag_part * cosine], -2
    )


def complex_mul(left, right):
    return jnp.stack(
        [
            left[..., 0, :] * right[..., 0, :] - left[..., 1, :] * right[..., 1, :],
            left[..., 0, :] * right[..., 1, :] + left[..., 1, :] * right[..., 0, :],
        ],
        -2,
    )


def conj_mul(left, right):
    return jnp.stack(
        [
            left[..., 0, :] * right[..., 0, :] + left[..., 1, :] * right[..., 1, :],
            left[..., 0, :] * right[..., 1, :] - left[..., 1, :] * right[..., 0, :],
        ],
        -2,
    )


def shear_rows(values, shift, sign):
    length = values.shape[-1]
    lines = values.shape[0]
    forward = block(dft_parts(length, length, length, -1.0))
    inverse = block(dft_parts(length, length, length, 1.0))
    spectra = jnp.dot(
        values.reshape(lines, 2 * length),
        forward,
        precision=PRECISE,
        preferred_element_type=jnp.float32,
    )
    phase = sign * -2.0 * jnp.pi / length * shift[:, None] * signed_freq(length)[None, :]
    spectra = turn_phase(spectra.reshape(lines, 2, length), phase)
    result = jnp.dot(
        spectra.reshape(lines, 2 * length),
        inverse,
        precision=PRECISE,
        preferred_element_type=jnp.float32,
    )
    return result.reshape(lines, 2, length)


def shear_columns(values, shift, sign):
    length = values.shape[1]
    forward = quad(*dft_parts(length, length, length, -1.0))
    inverse = quad(*dft_parts(length, length, length, 1.0))
    spectra = jnp.einsum("oaib,zbix->zaox", forward, values, precision=PRECISE)
    phase = sign * -2.0 * jnp.pi / length * signed_freq(length)[:, None] * shift[None, :]
    spectra = turn_phase(spectra, phase)
    return jnp.einsum("oaib,zbix->zaox", inverse, spectra, precision=PRECISE)


def geometry(motion_row):
    offsets = motion_row.astype(jnp.float32) - (LEVELS - 1) / 2.0
    angle = offsets[0] * ANGLE_STEP
    return (-jnp.tan(angle / 2.0), jnp.sin(angle), offsets[1] * SHIFT_STEP, offsets[2] * SHIFT_STEP)


def line_table(mask_row):
    cosine, sine_part = dft_parts(NY, NY, NY, 1.0)
    weight = mask_row.astype(jnp.float32)[:, None]
    real_part = jnp.dot(cosine.T, weight * cosine, precision=PRECISE) + jnp.dot(
        sine_part.T, weight * sine_part, precision=PRECISE
    )
    imag_part = jnp.dot(sine_part.T, weight * cosine, precision=PRECISE) - jnp.dot(
        cosine.T, weight * sine_part, precision=PRECISE
    )
    return quad(real_part, imag_part).astype(jnp.bfloat16)


def to_columns(values):
    return lax.all_to_all(values, "space", split_axis=2, concat_axis=0, tiled=True)


def to_rows(values):
    return lax.all_to_all(values, "space", split_axis=0, concat_axis=2, tiled=True)


def rotate_shards(values, motion_row, sign, device_rank, devices):
    slope, tilt, shift_x, shift_y = geometry(motion_row)
    lines = values.shape[0]
    width = values.shape[2]
    across = ((device_rank * lines + jnp.arange(lines, dtype=jnp.int32)) % NY).astype(
        jnp.float32
    ) - NY / 2.0

    def column_pass(current):
        columns = width // devices
        along = (device_rank * columns + jnp.arange(columns, dtype=jnp.int32)).astype(
            jnp.float32
        ) - width / 2.0
        gathered = to_columns(current)
        all_lines = gathered.shape[0]
        view_slices = gathered.reshape(all_lines // NY, NY, 2, columns)
        sheared = shear_columns(view_slices, tilt * along + shift_y, sign).reshape(
            all_lines, 2, columns
        )
        return to_rows(sheared)

    if sign > 0:
        current = shear_rows(values, slope * across + shift_x, 1.0)
        current = column_pass(current)
        return shear_rows(current, slope * across, 1.0)
    current = shear_rows(values, slope * across, -1.0)
    current = column_pass(current)
    return shear_rows(current, slope * across + shift_x, -1.0)


def gather_slice(values, bit_count, device_rank):
    for bit_index in range(bit_count):
        partner = from_partner(values, "space", bit_index)
        low_side = device_rank >> bit_index & 1 == 0
        values = jnp.where(
            low_side, jnp.concatenate([values, partner], 0), jnp.concatenate([partner, values], 0)
        )
    return values


def sum_slice(values, bit_count, device_rank):
    for bit_index in reversed(range(bit_count)):
        half_rows = values.shape[0] // 2
        low_side = device_rank >> bit_index & 1 == 0
        kept_part = jnp.where(low_side, values[:half_rows], values[half_rows:])
        sent_part = jnp.where(low_side, values[half_rows:], values[:half_rows])
        values = kept_part + from_partner(sent_part, "space", bit_index)
    return values


def regroup_coils(coil_maps, bit_count, device_rank):
    group_size = 1 << bit_count
    pieces = coil_maps.reshape((group_size, coil_maps.shape[0] // group_size) + coil_maps.shape[1:])
    for bit_index in range(bit_count):
        old_shape = pieces.shape
        halves = pieces.reshape((group_size >> bit_index + 1, 2, 1 << bit_index) + old_shape[1:])
        low_side = device_rank >> bit_index & 1 == 0
        kept_part = jnp.where(low_side, halves[:, 0], halves[:, 1])
        sent_part = jnp.where(low_side, halves[:, 1], halves[:, 0])
        partner = from_partner(sent_part, "space", bit_index)
        pieces = jnp.stack(
            [jnp.where(low_side, kept_part, partner), jnp.where(low_side, partner, kept_part)], 1
        ).reshape(old_shape)
    moved = jnp.moveaxis(pieces, 0, 1)
    return moved.reshape((moved.shape[0], group_size * coil_maps.shape[1]) + coil_maps.shape[2:])


def encode(coils, slab_image, psf_values, pad_table):
    coil_count, lines, _, width = coils.shape
    readout = psf_values.shape[1]
    coil_image = complex_mul(coils.astype(jnp.float32), slab_image[None]).astype(jnp.bfloat16)
    spectra = jnp.dot(
        coil_image.reshape(coil_count * lines, 2 * width),
        pad_table,
        preferred_element_type=jnp.float32,
    )
    return turn_phase(spectra.reshape(coil_count, lines, 2, readout), psf_values[None]).astype(
        jnp.bfloat16
    )


def project(projector, waved):
    coil_count, lines, _, columns = waved.shape
    view_slices = waved.reshape(coil_count, lines // NY, NY, 2, columns)
    projected = jnp.einsum(
        "oaib,czbik->czaok", projector, view_slices, preferred_element_type=jnp.float32
    )
    return projected.astype(jnp.bfloat16).reshape(waved.shape)


def decode(coils, projected, psf_values, crop_table):
    coil_count, lines, _, readout = projected.shape
    width = coils.shape[3]
    unwaved = turn_phase(projected.astype(jnp.float32), -psf_values[None]).astype(jnp.bfloat16)
    back = jnp.dot(
        unwaved.reshape(coil_count * lines, 2 * readout),
        crop_table,
        preferred_element_type=jnp.float32,
    )
    return jnp.sum(
        conj_mul(coils.astype(jnp.float32), back.reshape(coil_count, lines, 2, width)), 0
    )


def round_up(size, step):
    return -(-size // step) * step


def host_dft(size_in, size_out, modulus):
    turns = np.outer(np.arange(size_in), np.arange(size_out)) % modulus
    angle = turns.astype(np.float64) * (2.0 * np.pi / modulus)
    factor = float(modulus) ** -0.5
    return np.cos(angle) * factor, np.sin(angle) * factor


def placed(table, rows, columns):
    out = np.zeros((rows, columns), np.float64)
    out[: table.shape[0], : table.shape[1]] = table
    return out


def split_table(table):
    high = table.astype(np.float32).astype(jnp.bfloat16)
    low = (table - high.astype(np.float64)).astype(np.float32).astype(jnp.bfloat16)
    return np.stack([high, low])


def host_tables(width, height, readout):
    wide, tall, deep = round_up(width, 256), round_up(height, 256), round_up(readout, 128)
    cosine, sine = host_dft(width, readout, readout)
    pad = np.concatenate([placed(cosine, width, deep), placed(sine, width, deep)], 1)
    crop = np.concatenate([placed(cosine.T, deep, wide), placed(sine.T, deep, wide)], 1)
    row_parts = [placed(part, wide, wide) for part in host_dft(width, width, width)]
    column_parts = [placed(part, tall, tall) for part in host_dft(height, height, height)]
    return (
        pad.astype(np.float32).astype(jnp.bfloat16),
        crop.astype(np.float32).astype(jnp.bfloat16),
        split_table(np.concatenate(row_parts, 1)),
        split_table(np.stack(column_parts)),
    )


SINE = [(-1.0) ** n / math.factorial(2 * n + 1) for n in range(6)]
COSINE = [(-1.0) ** n / math.factorial(2 * n) for n in range(7)]


def poly(square, coefficients):
    value = jnp.full_like(square, coefficients[-1])
    for coefficient in reversed(coefficients[:-1]):
        value = value * square + coefficient
    return value


def cos_sin_of_half(half):
    square = half * half
    sine = half * poly(square, SINE)
    cosine = poly(square, COSINE)
    return 1.0 - 2.0 * sine * sine, 2.0 * sine * cosine


def cos_sin_turns(turns):
    rest = turns - jnp.floor(turns + 0.5)
    return cos_sin_of_half(rest * math.pi)


def split_value(value):
    high = value.astype(jnp.bfloat16)
    return high, (value - high.astype(jnp.float32)).astype(jnp.bfloat16)


def mxu(left, right):
    return jnp.dot(left, right, preferred_element_type=jnp.float32)


def slice_kernel(
    height,
    width,
    readout,
    motion_ref,
    mask_ref,
    image_ref,
    coil_ref,
    psf_ref,
    pad_ref,
    crop_ref,
    row_ref,
    column_ref,
    out_ref,
    pad_s,
    crop_s,
    cosine_s,
    sine_s,
    table_s,
    waved_s,
    unwaved_s,
    rotated_s,
    sum_s,
    phase_s,
):
    rows, wide = image_ref.shape[1:]
    deep = cosine_s.shape[1]
    tall = column_ref.shape[2]
    coils = coil_ref.shape[0]

    pad_s[...] = jnp.zeros_like(pad_s)
    pad_s[0:width, :deep] = pad_ref[:, :deep]
    pad_s[0:width, deep:] = -pad_ref[:, deep:]
    pad_s[wide : wide + width, :deep] = pad_ref[:, deep:]
    pad_s[wide : wide + width, deep:] = pad_ref[:, :deep]
    crop_s[0:deep, :] = crop_ref[...]
    crop_s[deep:, :wide] = -crop_ref[:, wide:]
    crop_s[deep:, wide:] = crop_ref[:, :wide]

    cosine_s[...] = jnp.zeros_like(cosine_s)
    sine_s[...] = jnp.zeros_like(sine_s)
    turn_cosine, turn_sine = cos_sin_of_half(psf_ref[...] * 0.5)
    cosine_s[:height, :readout] = turn_cosine
    sine_s[:height, :readout] = turn_sine

    theta = (motion_ref[0, 0].astype(jnp.float32) - (LEVELS - 1) / 2.0) * ANGLE_STEP
    shift_x = (motion_ref[0, 1].astype(jnp.float32) - (LEVELS - 1) / 2.0) * SHIFT_STEP
    shift_y = (motion_ref[0, 2].astype(jnp.float32) - (LEVELS - 1) / 2.0) * SHIFT_STEP
    half = theta * 0.5
    half_square = half * half
    slope = -half * (
        1.0
        + half_square
        * (1.0 / 3.0 + half_square * (2.0 / 15.0 + half_square * (17.0 / 315.0)))
    )
    square = theta * theta
    tilt = theta * (
        1.0 - square * (1.0 / 6.0 - square * (1.0 / 120.0 - square * (1.0 / 5040.0)))
    )

    line = lax.broadcasted_iota(jnp.int32, (rows, wide), 0)
    place = lax.broadcasted_iota(jnp.int32, (rows, wide), 1)
    across = line.astype(jnp.float32) - height / 2.0
    along = place.astype(jnp.float32) - width / 2.0
    place_freq = jnp.where(place < width // 2, place, place - width).astype(jnp.float32) / width
    line_freq = jnp.where(line < height // 2, line, line - height).astype(jnp.float32) / height
    for which, turns in enumerate(
        [
            (slope * across + shift_x) * place_freq,
            (tilt * along + shift_y) * line_freq,
            (slope * across) * place_freq,
        ]
    ):
        cosine, sine = cos_sin_turns(turns)
        phase_s[2 * which] = cosine
        phase_s[2 * which + 1] = sine

    def row_dft(real, imag):
        high, low = split_value(jnp.concatenate([real, imag], 0))
        table_high, table_low = row_ref[0], row_ref[1]
        out = mxu(high, table_high) + (mxu(low, table_high) + mxu(high, table_low))
        return (
            out[:rows, :wide] + out[rows:, wide:],
            out[rows:, :wide] - out[:rows, wide:],
        )

    def column_dft(real, imag):
        stacked = jnp.concatenate([real, imag], 1)
        stacked = jnp.concatenate(
            [stacked, jnp.zeros((tall - rows, 2 * wide), jnp.float32)], 0
        )
        high, low = split_value(stacked)

        def apply(which):
            table_high = column_ref[0, which, :rows]
            table_low = column_ref[1, which, :rows]
            return mxu(table_high, high) + (mxu(table_high, low) + mxu(table_low, high))

        by_cosine, by_sine = apply(0), apply(1)
        return (
            by_cosine[:, :wide] + by_sine[:, wide:],
            by_cosine[:, wide:] - by_sine[:, :wide],
        )

    def shear(dft, real, imag, which, sign):
        cosine = phase_s[2 * which]
        sine = phase_s[2 * which + 1]
        real, imag = dft(real, imag)
        turned = real * cosine + sign * (imag * sine)
        turned_negative = sign * (real * sine) - imag * cosine
        real, imag = dft(turned, turned_negative)
        return real, -imag

    real, imag = image_ref[0], image_ref[1]
    real, imag = shear(row_dft, real, imag, 0, 1.0)
    real, imag = shear(column_dft, real, imag, 1, 1.0)
    real, imag = shear(row_dft, real, imag, 2, 1.0)
    rotated_s[0] = real
    rotated_s[1] = imag

    weight = mask_ref[...].astype(jnp.float32)

    def masked(part, which):
        return (column_ref[part, which, :rows].astype(jnp.float32) * weight).astype(jnp.bfloat16)

    def triple(left, right):
        right_high, right_low = column_ref[0, right], column_ref[1, right]
        left_high, left_low = masked(0, left), masked(1, left)
        return mxu(left_high, right_high) + (
            mxu(left_low, right_high) + mxu(left_high, right_low)
        )

    table_real = triple(0, 0) + triple(1, 1)
    table_imag = triple(1, 0) - triple(0, 1)
    table_s[:rows, :tall] = table_real.astype(jnp.bfloat16)
    table_s[:rows, tall:] = (-table_imag).astype(jnp.bfloat16)
    table_s[rows:, :tall] = table_imag.astype(jnp.bfloat16)
    table_s[rows:, tall:] = table_real.astype(jnp.bfloat16)
    waved_s[...] = jnp.zeros_like(waved_s)
    sum_s[...] = jnp.zeros_like(sum_s)

    pair = 2 if coils % 2 == 0 else 1

    def some_coils(step, carry):
        for at in range(pair):
            coil = step * pair + at
            coil_real = coil_ref[coil, 0].astype(jnp.float32)
            coil_imag = coil_ref[coil, 1].astype(jnp.float32)
            real, imag = rotated_s[0], rotated_s[1]
            coil_image = jnp.concatenate(
                [
                    (coil_real * real - coil_imag * imag).astype(jnp.bfloat16),
                    (coil_real * imag + coil_imag * real).astype(jnp.bfloat16),
                ],
                1,
            )
            spectra = mxu(coil_image, pad_s[...])
            real, imag = spectra[:, :deep], spectra[:, deep:]
            cosine, sine = cosine_s[...], sine_s[...]
            columns = slice(at * deep, (at + 1) * deep)
            waved_s[:rows, columns] = (real * cosine - imag * sine).astype(jnp.bfloat16)
            waved_s[tall : tall + rows, columns] = (real * sine + imag * cosine).astype(
                jnp.bfloat16
            )
        for at in range(pair):
            coil = step * pair + at
            columns = slice(at * deep, (at + 1) * deep)
            projected = mxu(table_s[...], waved_s[:, columns])
            real, imag = projected[:rows], projected[rows:]
            cosine, sine = cosine_s[...], sine_s[...]
            unwaved_s[at, :, :deep] = (real * cosine + imag * sine).astype(jnp.bfloat16)
            unwaved_s[at, :, deep:] = (imag * cosine - real * sine).astype(jnp.bfloat16)
        for at in range(pair):
            coil = step * pair + at
            back = mxu(unwaved_s[at], crop_s[...])
            real, imag = back[:, :wide], back[:, wide:]
            coil_real = coil_ref[coil, 0].astype(jnp.float32)
            coil_imag = coil_ref[coil, 1].astype(jnp.float32)
            sum_s[0] += coil_real * real + coil_imag * imag
            sum_s[1] += coil_real * imag - coil_imag * real
        return carry

    lax.fori_loop(0, coils // pair, some_coils, 0)

    real, imag = sum_s[0], sum_s[1]
    real, imag = shear(row_dft, real, imag, 2, -1.0)
    real, imag = shear(column_dft, real, imag, 1, -1.0)
    real, imag = shear(row_dft, real, imag, 0, -1.0)
    out_ref[0] = real
    out_ref[1] = imag


def partner_kernel(own_ref, out_ref, other_s, send_sem, recv_sem):
    partner = {"shot": 1 - lax.axis_index("shot")}
    barrier = pltpu.get_barrier_semaphore()
    pl.semaphore_signal(
        barrier, inc=1, device_id=partner, device_id_type=pl.DeviceIdType.MESH
    )
    pl.semaphore_wait(barrier, 1)
    copy = pltpu.make_async_remote_copy(
        src_ref=own_ref,
        dst_ref=other_s,
        send_sem=send_sem,
        recv_sem=recv_sem,
        device_id=partner,
        device_id_type=pl.DeviceIdType.MESH,
    )
    copy.start()
    copy.wait()
    out_ref[...] = own_ref[...] + other_s[...]


def whole_slice(image, coil_maps, psf_phase, line_mask, motion):
    height, width, readout = image.shape[0], image.shape[2], psf_phase.shape[1]
    coils = coil_maps.shape[0]
    rows, wide = round_up(height, 16), round_up(width, 256)
    tall, deep = round_up(height, 256), round_up(readout, 128)
    edges = (0, rows - height, 0), (0, wide - width, 0)
    zero = jnp.zeros((), jnp.float32)
    planes = lax.pad(jnp.swapaxes(image, 0, 1), zero, ((0, 0, 0),) + edges)
    coil_planes = lax.pad(
        jnp.swapaxes(coil_maps, 1, 2),
        zero.astype(coil_maps.dtype),
        ((0, 0, 0), (0, 0, 0)) + edges,
    )
    mask = lax.pad(line_mask, jnp.int32(0), ((0, 0, 0), (0, tall - height, 0)))
    tables = [jnp.asarray(table) for table in host_tables(width, height, readout)]
    vmem = pl.BlockSpec(memory_space=pltpu.VMEM)
    own = pl.pallas_call(
        functools.partial(slice_kernel, height, width, readout),
        out_shape=jax.ShapeDtypeStruct((2, rows, wide), jnp.float32),
        in_specs=[pl.BlockSpec(memory_space=pltpu.SMEM)] + [vmem] * 8,
        out_specs=vmem,
        scratch_shapes=[
            pltpu.VMEM((2 * wide, 2 * deep), jnp.bfloat16),
            pltpu.VMEM((2 * deep, 2 * wide), jnp.bfloat16),
            pltpu.VMEM((rows, deep), jnp.float32),
            pltpu.VMEM((rows, deep), jnp.float32),
            pltpu.VMEM((2 * rows, 2 * tall), jnp.bfloat16),
            pltpu.VMEM((2 * tall, 2 * deep), jnp.bfloat16),
            pltpu.VMEM((2, rows, 2 * deep), jnp.bfloat16),
            pltpu.VMEM((2, rows, wide), jnp.float32),
            pltpu.VMEM((2, rows, wide), jnp.float32),
            pltpu.VMEM((6, rows, wide), jnp.float32),
        ],
        compiler_params=pltpu.CompilerParams(vmem_limit_bytes=60 * 1024 * 1024),
        name="slice_kernel",
    )(motion, mask, planes, coil_planes, psf_phase, *tables)
    both = pl.pallas_call(
        partner_kernel,
        out_shape=jax.ShapeDtypeStruct(own.shape, own.dtype),
        in_specs=[vmem],
        out_specs=vmem,
        scratch_shapes=[
            pltpu.VMEM(own.shape, own.dtype),
            pltpu.SemaphoreType.DMA,
            pltpu.SemaphoreType.DMA,
        ],
        compiler_params=pltpu.CompilerParams(collective_id=0, has_side_effects=True),
        name="partner_kernel",
    )(own)
    return jnp.swapaxes(both[:, :height, :width], 0, 1)


def on_device(image, coil_maps, psf_phase, line_mask, motion):
    lines = image.shape[0]
    width = image.shape[2]
    readout = psf_phase.shape[1]
    if lines == NY and lax.axis_size("shot") == 2:
        return whole_slice(image, coil_maps, psf_phase, line_mask, motion)
    devices = lax.axis_size("space")
    device_rank = lax.axis_index("space")
    pad_table = block(dft_parts(width, readout, readout, -1.0)).astype(jnp.bfloat16)
    crop_table = block(dft_parts(readout, width, readout, 1.0)).astype(jnp.bfloat16)
    group_size = max(1, NY // lines)
    bit_count = group_size.bit_length() - 1
    own_coils = regroup_coils(coil_maps, bit_count, device_rank)
    own_psf = gather_slice(psf_phase, bit_count, device_rank)
    projector = line_table(line_mask[0])
    rotated = rotate_shards(image, motion[0], 1, device_rank, devices)
    slab_image = gather_slice(rotated, bit_count, device_rank)
    waved = encode(own_coils, slab_image, own_psf, pad_table)
    partial_sum = decode(own_coils, project(projector, waved), own_psf, crop_table)
    combined = sum_slice(partial_sum, bit_count, device_rank)
    running = rotate_shards(combined, motion[0], -1, device_rank, devices)
    return lax.psum(running, "shot")


def solution(mesh):
    in_specs = (
        P(("parts", "space"), None, None),
        P(None, ("parts", "space"), None, None),
        P(("parts", "space"), None),
        P(("parts", "shot"), None),
        P(("parts", "shot"), None),
    )
    out_specs = P(("parts", "space"), None, None)
    return jax.shard_map(
        on_device, mesh=mesh, in_specs=in_specs, out_specs=out_specs, check_vma=False
    )
```

profile of v0, /device:TPU:7, one launch (start us, length us, event | category | flops | bytes accessed | tf_op | source)
XLA Modules:
  0.0 48.5 jit_solution(11324351530682945483)
XLA Ops:
  0.0 5.1 %copy.11 = bf16[16,200,2,192]{3,1,2,0:T(8,128)(2,1)S(1)} copy(bf16[16,200,2,192]{1,3,2,0:T(8,128)(2,1)} %param.10) | data formatting | bytes 4915200 | tf_op args[1]
  5.1 0.0 copy-start
  5.1 2.4 %pad.11.coil_ref = bf16[16,2,208,256]{3,2,1,0:T(8,128)(2,1)} pad(bf16[16,2,200,192]{3,2,1,0:T(8,128)(2,1)S(1)} %bitcast.4, bf16[]{:T(256)} %constant.6.clone.1), padding=0_0x0_0x0_8x0_64 | pad | bytes 5865474 | tf_op jit(solution)/shard_map/pad | solution.py:535
  7.5 1.2 %copy.10 = f32[200,2,192]{2,0,1:T(8,128)S(1)} copy(f32[200,2,192]{0,2,1:T(8,128)} %param.9) | data formatting | bytes 614400 | tf_op args[0]
  8.7 0.8 %pad.10.image_ref = f32[2,208,256]{2,1,0:T(8,128)} pad(f32[2,200,192]{2,1,0:T(8,128)S(1)} %bitcast.5, f32[]{:T(128)} %constant.5.clone.1), padding=0_0x0_8x0_64 | pad | bytes 733188 | tf_op jit(solution)/shard_map/pad | solution.py:534
  9.4 0.0 copy-done
  9.4 0.6 %pad.9.mask_ref = s32[1,256]{1,0:T(1,128)} pad(s32[1,200]{1,0:T(1,128)S(1)} %copy-done, s32[]{:T(128)} %constant.4.clone.1), padding=0_0x0_56 | pad | bytes 1828 | tf_op jit(solution)/shard_map/pad | solution.py:540
  10.0 32.6 %slice_kernel.1.own_ref = f32[2,208,256]{2,1,0:T(8,128)} custom-call(s32[1,3]{1,0:T(1,128)} %motion_ref.1, s32[1,256]{1,0:T(1,128)} %pad.9.mask_ref, f32[2,208,256]{2,1,0:T(8,128)} %pad.10.image_ref, bf16[16,2,208,256]{3,2,1,0:T(8,128)(2,1)} %pad.11.coil_ref, f32[200,576]{1,0:T(8,128)} %psf_ref.1, bf16[192,1280]{1,0:T(8,128)(2,1)} %constant.14.clone.pad_ref, ...), custom_call_target="tpu_custom_call" | custom-call | tf_op jit(solution)/shard_map/slice_kernel/pallas_call | solution.py:543
  42.6 3.9 %partner_kernel.1 = f32[2,208,256]{2,1,0:T(8,128)} custom-call(f32[2,208,256]{2,1,0:T(8,128)} %slice_kernel.1.own_ref), custom_call_target="tpu_custom_call" | custom-call | tf_op jit(solution)/shard_map/partner_kernel/pallas_call | solution.py:563
  46.5 1.0 %slice_bitcast_fusion = f32[200,2,192]{2,0,1:T(8,128)S(1)} fusion(f32[2,208,256]{2,1,0:T(8,128)} %partner_kernel.1), kind=kLoop, calls=%fused_computation | loop fusion | bytes 614400 | tf_op jit(solution)/shard_map/transpose | solution.py:576
  47.5 0.9 %copy.12 = f32[200,2,192]{0,2,1:T(8,128)} copy(f32[200,2,192]{2,0,1:T(8,128)S(1)} %slice_bitcast_fusion) | data formatting | bytes 614400 | tf_op jit(solution)/shard_map/transpose | solution.py:576
Async XLA Ops:
  5.1 4.4 %copy-start = (s32[1,200]{1,0:T(1,128)S(1)}, s32[1,200]{1,0:T(1,128)}, u32[]{:S(2)}) copy-start(s32[1,200]{1,0:T(1,128)} %param.12) | copy-start | bytes 2404
where the time goes:
time: 48.8 us; the launch traced here: 48.5 us
  Pallas kernels  36.5 us (75%)
  local copies, waits for them, and re-layouts  11.9 us (24%)
    pallas_call x1, Pallas kernels, whole_slice(): pl.pallas_call(functools.partial(slice_kernel, height, width, readout), o...  32.6 us
    unnamed x4, local copies, waits for them, and re-layouts  6.25 us
    pallas_call x1, Pallas kernels, whole_slice(): pl.pallas_call(partner_kernel, out_shape=jax.ShapeDtypeStruct(own.shape,...  3.91 us
    pad x1, local copies, waits for them, and re-layouts, whole_slice(): lax.pad(jnp.swapaxes(coil_maps, 1, 2), zero.astype(coil_maps.dtype), ((0,...  2.37 us
    transpose x2, local copies, waits for them, and re-layouts, whole_slice(): return jnp.swapaxes(both[:, :height, :width], 0, 1)  1.96 us

commit v1 on v0

--- a/solution.py
+++ b/solution.py
@@ -266,17 +266,16 @@
 
 
 def host_tables(width, height, readout):
-    wide, tall, deep = round_up(width, 256), round_up(height, 256), round_up(readout, 128)
-    cosine, sine = host_dft(width, readout, readout)
-    pad = np.concatenate([placed(cosine, width, deep), placed(sine, width, deep)], 1)
-    crop = np.concatenate([placed(cosine.T, deep, wide), placed(sine.T, deep, wide)], 1)
-    row_parts = [placed(part, wide, wide) for part in host_dft(width, width, width)]
+    tall = round_up(height, 256)
+    cosine, sine = host_dft(readout, width, readout)
+    encode_table = np.block([[cosine, sine], [-sine, cosine]])
+    row_parts = host_dft(width, width, width)
     column_parts = [placed(part, tall, tall) for part in host_dft(height, height, height)]
     return (
-        pad.astype(np.float32).astype(jnp.bfloat16),
-        crop.astype(np.float32).astype(jnp.bfloat16),
-        split_table(np.concatenate(row_parts, 1)),
-        split_table(np.stack(column_parts)),
+        encode_table.astype(np.float32).astype(jnp.bfloat16),
+        encode_table.T.astype(np.float32).astype(jnp.bfloat16),
+        split_table(np.concatenate(row_parts, 0)),
+        split_table(np.concatenate(column_parts, 1)),
     )
 
 
@@ -313,49 +312,52 @@
 
 
 def slice_kernel(
-    height,
-    width,
-    readout,
     motion_ref,
     mask_ref,
     image_ref,
-    coil_ref,
     psf_ref,
-    pad_ref,
-    crop_ref,
     row_ref,
     column_ref,
+    coil_hbm,
+    encode_hbm,
+    decode_hbm,
     out_ref,
-    pad_s,
-    crop_s,
+    coil_s,
+    encode_s,
+    decode_s,
+    psf_s,
+    mask_s,
     cosine_s,
     sine_s,
+    phase_s,
+    image_s,
     table_s,
+    coil_image_s,
     waved_s,
     unwaved_s,
-    rotated_s,
     sum_s,
-    phase_s,
+    copy_sems,
 ):
-    rows, wide = image_ref.shape[1:]
-    deep = cosine_s.shape[1]
-    tall = column_ref.shape[2]
-    coils = coil_ref.shape[0]
-
-    pad_s[...] = jnp.zeros_like(pad_s)
-    pad_s[0:width, :deep] = pad_ref[:, :deep]
-    pad_s[0:width, deep:] = -pad_ref[:, deep:]
-    pad_s[wide : wide + width, :deep] = pad_ref[:, deep:]
-    pad_s[wide : wide + width, deep:] = pad_ref[:, :deep]
-    crop_s[0:deep, :] = crop_ref[...]
-    crop_s[deep:, :wide] = -crop_ref[:, wide:]
-    crop_s[deep:, wide:] = crop_ref[:, :wide]
-
-    cosine_s[...] = jnp.zeros_like(cosine_s)
-    sine_s[...] = jnp.zeros_like(sine_s)
-    turn_cosine, turn_sine = cos_sin_of_half(psf_ref[...] * 0.5)
-    cosine_s[:height, :readout] = turn_cosine
-    sine_s[:height, :readout] = turn_sine
+    _, width, height = image_ref.shape
+    readout = psf_ref.shape[1]
+    tall = column_ref.shape[1]
+    coils = coil_s.shape[0]
+
+    copies = [
+        pltpu.make_async_copy(source, target, copy_sems.at[at])
+        for at, (source, target) in enumerate(
+            [(coil_hbm, coil_s), (encode_hbm, encode_s), (decode_hbm, decode_s)]
+        )
+    ]
+    for copy in copies:
+        copy.start()
+
+    psf_s[...] = jnp.zeros_like(psf_s)
+    psf_s[:height, :readout] = psf_ref[...]
+    turned_psf = jnp.transpose(psf_s[...])[:readout]
+    turn_cosine, turn_sine = cos_sin_of_half(turned_psf * 0.5)
+    cosine_s[...] = turn_cosine
+    sine_s[...] = turn_sine
 
     theta = (motion_ref[0, 0].astype(jnp.float32) - (LEVELS - 1) / 2.0) * ANGLE_STEP
     shift_x = (motion_ref[0, 1].astype(jnp.float32) - (LEVELS - 1) / 2.0) * SHIFT_STEP
@@ -372,8 +374,8 @@
         1.0 - square * (1.0 / 6.0 - square * (1.0 / 120.0 - square * (1.0 / 5040.0)))
     )
 
-    line = lax.broadcasted_iota(jnp.int32, (rows, wide), 0)
-    place = lax.broadcasted_iota(jnp.int32, (rows, wide), 1)
+    place = lax.broadcasted_iota(jnp.int32, (width, tall), 0)
+    line = lax.broadcasted_iota(jnp.int32, (width, tall), 1)
     across = line.astype(jnp.float32) - height / 2.0
     along = place.astype(jnp.float32) - width / 2.0
     place_freq = jnp.where(place < width // 2, place, place - width).astype(jnp.float32) / width
@@ -390,30 +392,21 @@
         phase_s[2 * which + 1] = sine
 
     def row_dft(real, imag):
+        high, low = split_value(jnp.concatenate([real, imag], 1))
+        table_high, table_low = row_ref[0], row_ref[1]
+        out = mxu(table_high, high) + (mxu(table_high, low) + mxu(table_low, high))
+        return (
+            out[:width, :tall] + out[width:, tall:],
+            out[:width, tall:] - out[width:, :tall],
+        )
+
+    def column_dft(real, imag):
         high, low = split_value(jnp.concatenate([real, imag], 0))
-        table_high, table_low = row_ref[0], row_ref[1]
+        table_high, table_low = column_ref[0], column_ref[1]
         out = mxu(high, table_high) + (mxu(low, table_high) + mxu(high, table_low))
         return (
-            out[:rows, :wide] + out[rows:, wide:],
-            out[rows:, :wide] - out[:rows, wide:],
-        )
-
-    def column_dft(real, imag):
-        stacked = jnp.concatenate([real, imag], 1)
-        stacked = jnp.concatenate(
-            [stacked, jnp.zeros((tall - rows, 2 * wide), jnp.float32)], 0
-        )
-        high, low = split_value(stacked)
-
-        def apply(which):
-            table_high = column_ref[0, which, :rows]
-            table_low = column_ref[1, which, :rows]
-            return mxu(table_high, high) + (mxu(table_high, low) + mxu(table_low, high))
-
-        by_cosine, by_sine = apply(0), apply(1)
-        return (
-            by_cosine[:, :wide] + by_sine[:, wide:],
-            by_cosine[:, wide:] - by_sine[:, :wide],
+            out[:width, :tall] + out[width:, tall:],
+            out[width:, :tall] - out[:width, tall:],
         )
 
     def shear(dft, real, imag, which, sign):
@@ -425,20 +418,27 @@
         real, imag = dft(turned, turned_negative)
         return real, -imag
 
-    real, imag = image_ref[0], image_ref[1]
+    image_s[...] = jnp.zeros_like(image_s)
+    image_s[:, :, :height] = image_ref[...]
+    real, imag = image_s[0], image_s[1]
     real, imag = shear(row_dft, real, imag, 0, 1.0)
     real, imag = shear(column_dft, real, imag, 1, 1.0)
     real, imag = shear(row_dft, real, imag, 2, 1.0)
-    rotated_s[0] = real
-    rotated_s[1] = imag
-
-    weight = mask_ref[...].astype(jnp.float32)
+    image_s[0] = real
+    image_s[1] = imag
+
+    mask_s[...] = jnp.zeros_like(mask_s)
+    mask_s[:, :height] = mask_ref[...].astype(jnp.float32)
+    weight = mask_s[...]
+
+    def table_part(part, which):
+        return column_ref[part, :, which * tall : (which + 1) * tall]
 
     def masked(part, which):
-        return (column_ref[part, which, :rows].astype(jnp.float32) * weight).astype(jnp.bfloat16)
+        return (table_part(part, which).astype(jnp.float32) * weight).astype(jnp.bfloat16)
 
     def triple(left, right):
-        right_high, right_low = column_ref[0, right], column_ref[1, right]
+        right_high, right_low = table_part(0, right), table_part(1, right)
         left_high, left_low = masked(0, left), masked(1, left)
         return mxu(left_high, right_high) + (
             mxu(left_low, right_high) + mxu(left_high, right_low)
@@ -446,52 +446,49 @@
 
     table_real = triple(0, 0) + triple(1, 1)
     table_imag = triple(1, 0) - triple(0, 1)
-    table_s[:rows, :tall] = table_real.astype(jnp.bfloat16)
-    table_s[:rows, tall:] = (-table_imag).astype(jnp.bfloat16)
-    table_s[rows:, :tall] = table_imag.astype(jnp.bfloat16)
-    table_s[rows:, tall:] = table_real.astype(jnp.bfloat16)
-    waved_s[...] = jnp.zeros_like(waved_s)
+    table_s[:tall, :tall] = table_real.astype(jnp.bfloat16)
+    table_s[:tall, tall:] = (-table_imag).astype(jnp.bfloat16)
+    table_s[tall:, :tall] = table_imag.astype(jnp.bfloat16)
+    table_s[tall:, tall:] = table_real.astype(jnp.bfloat16)
+    coil_image_s[...] = jnp.zeros_like(coil_image_s)
     sum_s[...] = jnp.zeros_like(sum_s)
-
-    pair = 2 if coils % 2 == 0 else 1
+    for copy in copies:
+        copy.wait()
+
+    pair = coil_image_s.shape[0]
 
     def some_coils(step, carry):
         for at in range(pair):
             coil = step * pair + at
-            coil_real = coil_ref[coil, 0].astype(jnp.float32)
-            coil_imag = coil_ref[coil, 1].astype(jnp.float32)
-            real, imag = rotated_s[0], rotated_s[1]
-            coil_image = jnp.concatenate(
-                [
-                    (coil_real * real - coil_imag * imag).astype(jnp.bfloat16),
-                    (coil_real * imag + coil_imag * real).astype(jnp.bfloat16),
-                ],
-                1,
+            coil_real = coil_s[coil, 0].astype(jnp.float32)
+            coil_imag = coil_s[coil, 1].astype(jnp.float32)
+            real, imag = image_s[0, :, :height], image_s[1, :, :height]
+            coil_image_s[at, :width, :height] = (coil_real * real - coil_imag * imag).astype(
+                jnp.bfloat16
             )
-            spectra = mxu(coil_image, pad_s[...])
-            real, imag = spectra[:, :deep], spectra[:, deep:]
-            cosine, sine = cosine_s[...], sine_s[...]
-            columns = slice(at * deep, (at + 1) * deep)
-            waved_s[:rows, columns] = (real * cosine - imag * sine).astype(jnp.bfloat16)
-            waved_s[tall : tall + rows, columns] = (real * sine + imag * cosine).astype(
+            coil_image_s[at, width:, :height] = (coil_real * imag + coil_imag * real).astype(
                 jnp.bfloat16
             )
         for at in range(pair):
-            coil = step * pair + at
-            columns = slice(at * deep, (at + 1) * deep)
-            projected = mxu(table_s[...], waved_s[:, columns])
-            real, imag = projected[:rows], projected[rows:]
+            spectra = mxu(encode_s[...], coil_image_s[at])
+            real, imag = spectra[:readout], spectra[readout:]
             cosine, sine = cosine_s[...], sine_s[...]
-            unwaved_s[at, :, :deep] = (real * cosine + imag * sine).astype(jnp.bfloat16)
-            unwaved_s[at, :, deep:] = (imag * cosine - real * sine).astype(jnp.bfloat16)
+            waved_s[at, :, :tall] = (real * cosine - imag * sine).astype(jnp.bfloat16)
+            waved_s[at, :, tall:] = (real * sine + imag * cosine).astype(jnp.bfloat16)
+        for at in range(pair):
+            projected = mxu(waved_s[at], table_s[...])
+            real, imag = projected[:, :tall], projected[:, tall:]
+            cosine, sine = cosine_s[...], sine_s[...]
+            unwaved_s[at, :readout] = (real * cosine + imag * sine).astype(jnp.bfloat16)
+            unwaved_s[at, readout:] = (imag * cosine - real * sine).astype(jnp.bfloat16)
         for at in range(pair):
             coil = step * pair + at
-            back = mxu(unwaved_s[at], crop_s[...])
-            real, imag = back[:, :wide], back[:, wide:]
-            coil_real = coil_ref[coil, 0].astype(jnp.float32)
-            coil_imag = coil_ref[coil, 1].astype(jnp.float32)
-            sum_s[0] += coil_real * real + coil_imag * imag
-            sum_s[1] += coil_real * imag - coil_imag * real
+            back = mxu(decode_s[...], unwaved_s[at])
+            real, imag = back[:width, :height], back[width:, :height]
+            coil_real = coil_s[coil, 0].astype(jnp.float32)
+            coil_imag = coil_s[coil, 1].astype(jnp.float32)
+            sum_s[0, :, :height] += coil_real * real + coil_imag * imag
+            sum_s[1, :, :height] += coil_real * imag - coil_imag * real
         return carry
 
     lax.fori_loop(0, coils // pair, some_coils, 0)
@@ -500,11 +497,11 @@
     real, imag = shear(row_dft, real, imag, 2, -1.0)
     real, imag = shear(column_dft, real, imag, 1, -1.0)
     real, imag = shear(row_dft, real, imag, 0, -1.0)
-    out_ref[0] = real
-    out_ref[1] = imag
-
-
-def partner_kernel(own_ref, out_ref, other_s, send_sem, recv_sem):
+    out_ref[0] = real[:, :height]
+    out_ref[1] = imag[:, :height]
+
+
+def partner_kernel(own_ref, other_ref, send_sem, recv_sem):
     partner = {"shot": 1 - lax.axis_index("shot")}
     barrier = pltpu.get_barrier_semaphore()
     pl.semaphore_signal(
@@ -513,7 +510,7 @@
     pl.semaphore_wait(barrier, 1)
     copy = pltpu.make_async_remote_copy(
         src_ref=own_ref,
-        dst_ref=other_s,
+        dst_ref=other_ref,
         send_sem=send_sem,
         recv_sem=recv_sem,
         device_id=partner,
@@ -521,59 +518,65 @@
     )
     copy.start()
     copy.wait()
-    out_ref[...] = own_ref[...] + other_s[...]
 
 
 def whole_slice(image, coil_maps, psf_phase, line_mask, motion):
     height, width, readout = image.shape[0], image.shape[2], psf_phase.shape[1]
     coils = coil_maps.shape[0]
-    rows, wide = round_up(height, 16), round_up(width, 256)
-    tall, deep = round_up(height, 256), round_up(readout, 128)
-    edges = (0, rows - height, 0), (0, wide - width, 0)
-    zero = jnp.zeros((), jnp.float32)
-    planes = lax.pad(jnp.swapaxes(image, 0, 1), zero, ((0, 0, 0),) + edges)
-    coil_planes = lax.pad(
-        jnp.swapaxes(coil_maps, 1, 2),
-        zero.astype(coil_maps.dtype),
-        ((0, 0, 0), (0, 0, 0)) + edges,
-    )
-    mask = lax.pad(line_mask, jnp.int32(0), ((0, 0, 0), (0, tall - height, 0)))
-    tables = [jnp.asarray(table) for table in host_tables(width, height, readout)]
+    tall = round_up(height, 256)
+    pair = 2 if coils % 2 == 0 else 1
+    planes = jnp.transpose(image, (1, 2, 0))
+    coil_planes = jnp.transpose(coil_maps, (0, 2, 3, 1))
+    encode_table, decode_table, row_table, column_table = [
+        jnp.asarray(table) for table in host_tables(width, height, readout)
+    ]
     vmem = pl.BlockSpec(memory_space=pltpu.VMEM)
+    anywhere = pl.BlockSpec(memory_space=pl.ANY)
     own = pl.pallas_call(
-        functools.partial(slice_kernel, height, width, readout),
-        out_shape=jax.ShapeDtypeStruct((2, rows, wide), jnp.float32),
-        in_specs=[pl.BlockSpec(memory_space=pltpu.SMEM)] + [vmem] * 8,
+        slice_kernel,
+        out_shape=jax.ShapeDtypeStruct((2, width, height), jnp.float32),
+        in_specs=[pl.BlockSpec(memory_space=pltpu.SMEM)] + [vmem] * 5 + [anywhere] * 3,
         out_specs=vmem,
         scratch_shapes=[
-            pltpu.VMEM((2 * wide, 2 * deep), jnp.bfloat16),
-            pltpu.VMEM((2 * deep, 2 * wide), jnp.bfloat16),
-            pltpu.VMEM((rows, deep), jnp.float32),
-            pltpu.VMEM((rows, deep), jnp.float32),
-            pltpu.VMEM((2 * rows, 2 * tall), jnp.bfloat16),
-            pltpu.VMEM((2 * tall, 2 * deep), jnp.bfloat16),
-            pltpu.VMEM((2, rows, 2 * deep), jnp.bfloat16),
-            pltpu.VMEM((2, rows, wide), jnp.float32),
-            pltpu.VMEM((2, rows, wide), jnp.float32),
-            pltpu.VMEM((6, rows, wide), jnp.float32),
+            pltpu.VMEM(coil_planes.shape, coil_planes.dtype),
+            pltpu.VMEM(encode_table.shape, jnp.bfloat16),
+            pltpu.VMEM(decode_table.shape, jnp.bfloat16),
+            pltpu.VMEM((tall, round_up(readout, 128)), jnp.float32),
+            pltpu.VMEM((1, tall), jnp.float32),
+            pltpu.VMEM((readout, tall), jnp.float32),
+            pltpu.VMEM((readout, tall), jnp.float32),
+            pltpu.VMEM((6, width, tall), jnp.float32),
+            pltpu.VMEM((2, width, tall), jnp.float32),
+            pltpu.VMEM((2 * tall, 2 * tall), jnp.bfloat16),
+            pltpu.VMEM((pair, 2 * width, tall), jnp.bfloat16),
+            pltpu.VMEM((pair, readout, 2 * tall), jnp.bfloat16),
+            pltpu.VMEM((pair, 2 * readout, tall), jnp.bfloat16),
+            pltpu.VMEM((2, width, tall), jnp.float32),
+            pltpu.SemaphoreType.DMA((3,)),
         ],
-        compiler_params=pltpu.CompilerParams(vmem_limit_bytes=60 * 1024 * 1024),
+        compiler_params=pltpu.CompilerParams(vmem_limit_bytes=56 * 1024 * 1024),
         name="slice_kernel",
-    )(motion, mask, planes, coil_planes, psf_phase, *tables)
-    both = pl.pallas_call(
+    )(
+        motion,
+        line_mask,
+        planes,
+        psf_phase,
+        row_table,
+        column_table,
+        coil_planes,
+        encode_table,
+        decode_table,
+    )
+    other = pl.pallas_call(
         partner_kernel,
         out_shape=jax.ShapeDtypeStruct(own.shape, own.dtype),
         in_specs=[vmem],
         out_specs=vmem,
-        scratch_shapes=[
-            pltpu.VMEM(own.shape, own.dtype),
-            pltpu.SemaphoreType.DMA,
-            pltpu.SemaphoreType.DMA,
-        ],
+        scratch_shapes=[pltpu.SemaphoreType.DMA, pltpu.SemaphoreType.DMA],
         compiler_params=pltpu.CompilerParams(collective_id=0, has_side_effects=True),
         name="partner_kernel",
     )(own)
-    return jnp.swapaxes(both[:, :height, :width], 0, 1)
+    return jnp.transpose(own + other, (2, 0, 1))
 
 
 def on_device(image, coil_maps, psf_phase, line_mask, motion):

time: 48.8 us -> 36.4 us (0.75)
  local copies, waits for them, and re-layouts: 11.9 us -> 0 us
  Pallas kernels: 36.5 us -> 34.3 us
  other arithmetic: 0 us -> 1.91 us
    unnamed x4 -> x0, local copies, waits for them, and re-layouts: 6.25 us -> none
    pad x3 -> x0, local copies, waits for them, and re-layouts: 3.73 us -> none  [the longest x1 2.37 us: whole_slice(): lax.pad(jnp.swapaxes(coil_maps, 1, 2), zero.astype(coil_maps.dtype), ((0,...]
    pallas_call x1, Pallas kernels: 32.6 us -> 30.5 us  [whole_slice(): pl.pallas_call(slice_kernel, out_shape=jax.ShapeDtypeStruct((2, width, he...]
    transpose x2 -> x0, local copies, waits for them, and re-layouts: 1.96 us -> none  [whole_slice(): return jnp.swapaxes(both[:, :height, :width], 0, 1)]
    transpose x0 -> x1, other arithmetic: none -> 1.91 us  [whole_slice(): return jnp.transpose(own + other, (2, 0, 1))]
where the time goes in v1:
time: 36.4 us; the launch traced here: 36.2 us
  Pallas kernels  34.3 us (94%)
  other arithmetic  1.91 us (5%)
    pallas_call x1, Pallas kernels, whole_slice(): pl.pallas_call(slice_kernel, out_shape=jax.ShapeDtypeStruct((2, width, he...  30.5 us
    pallas_call x1, Pallas kernels, whole_slice(): pl.pallas_call(partner_kernel, out_shape=jax.ShapeDtypeStruct(own.shape,...  3.79 us
    transpose x1, other arithmetic, whole_slice(): return jnp.transpose(own + other, (2, 0, 1))  1.91 us

profile of v1, /device:TPU:7, one launch (start us, length us, event | category | flops | bytes accessed | tf_op | source)
XLA Modules:
  0.0 36.2 jit_solution(2841613674843563319)
XLA Ops:
  0.0 30.5 %slice_kernel.1.own_ref = f32[2,192,200]{2,1,0:T(8,128)} custom-call(s32[1,3]{1,0:T(1,128)} %motion_ref.1, s32[1,200]{1,0:T(1,128)} %mask_ref.1, f32[2,192,200]{2,1,0:T(8,128)} %bitcast.5, f32[200,576]{1,0:T(8,128)} %psf_ref.1, bf16[2,384,192]{2,1,0:T(8,128)(2,1)} %constant.10.clone.row_ref, bf16[2,256,512]{2,1,0:T(8,128)(2,1)} %constant.11.clone.column_ref, ...), custom_call_target="tpu_custom_call" | custom-call | tf_op jit(solution)/shard_map/slice_kernel/pallas_call | solution.py:535
  30.5 3.8 %partner_kernel.1 = f32[2,192,200]{2,1,0:T(8,128)} custom-call(f32[2,192,200]{2,1,0:T(8,128)} %slice_kernel.1.own_ref), custom_call_target="tpu_custom_call" | custom-call | tf_op jit(solution)/shard_map/partner_kernel/pallas_call | solution.py:570
  34.3 1.9 %add_bitcast_fusion = f32[200,2,192]{0,2,1:T(8,128)} fusion(f32[2,192,200]{2,1,0:T(8,128)} %slice_kernel.1.own_ref, f32[2,192,200]{2,1,0:T(8,128)} %partner_kernel.1), kind=kLoop, calls=%fused_computation | loop fusion | flops 76800 | bytes 921600 | tf_op jit(solution)/shard_map/transpose | solution.py:579

commit v2 on v1

--- a/solution.py
+++ b/solution.py
@@ -336,6 +336,7 @@
     waved_s,
     unwaved_s,
     sum_s,
+    other_s,
     copy_sems,
 ):
     _, width, height = image_ref.shape
@@ -351,6 +352,11 @@
     ]
     for copy in copies:
         copy.start()
+    partner = {"shot": 1 - lax.axis_index("shot")}
+    barrier = pltpu.get_barrier_semaphore()
+    pl.semaphore_signal(
+        barrier, inc=1, device_id=partner, device_id_type=pl.DeviceIdType.MESH
+    )
 
     psf_s[...] = jnp.zeros_like(psf_s)
     psf_s[:height, :readout] = psf_ref[...]
@@ -497,27 +503,20 @@
     real, imag = shear(row_dft, real, imag, 2, -1.0)
     real, imag = shear(column_dft, real, imag, 1, -1.0)
     real, imag = shear(row_dft, real, imag, 0, -1.0)
-    out_ref[0] = real[:, :height]
-    out_ref[1] = imag[:, :height]
-
-
-def partner_kernel(own_ref, other_ref, send_sem, recv_sem):
-    partner = {"shot": 1 - lax.axis_index("shot")}
-    barrier = pltpu.get_barrier_semaphore()
-    pl.semaphore_signal(
-        barrier, inc=1, device_id=partner, device_id_type=pl.DeviceIdType.MESH
-    )
+    sum_s[0] = real
+    sum_s[1] = imag
     pl.semaphore_wait(barrier, 1)
     copy = pltpu.make_async_remote_copy(
-        src_ref=own_ref,
-        dst_ref=other_ref,
-        send_sem=send_sem,
-        recv_sem=recv_sem,
+        src_ref=sum_s,
+        dst_ref=other_s,
+        send_sem=copy_sems.at[3],
+        recv_sem=copy_sems.at[4],
         device_id=partner,
         device_id_type=pl.DeviceIdType.MESH,
     )
     copy.start()
     copy.wait()
+    out_ref[...] = (sum_s[...] + other_s[...])[:, :, :height]
 
 
 def whole_slice(image, coil_maps, psf_phase, line_mask, motion):
@@ -532,7 +531,7 @@
     ]
     vmem = pl.BlockSpec(memory_space=pltpu.VMEM)
     anywhere = pl.BlockSpec(memory_space=pl.ANY)
-    own = pl.pallas_call(
+    total = pl.pallas_call(
         slice_kernel,
         out_shape=jax.ShapeDtypeStruct((2, width, height), jnp.float32),
         in_specs=[pl.BlockSpec(memory_space=pltpu.SMEM)] + [vmem] * 5 + [anywhere] * 3,
@@ -552,9 +551,12 @@
             pltpu.VMEM((pair, readout, 2 * tall), jnp.bfloat16),
             pltpu.VMEM((pair, 2 * readout, tall), jnp.bfloat16),
             pltpu.VMEM((2, width, tall), jnp.float32),
-            pltpu.SemaphoreType.DMA((3,)),
+            pltpu.VMEM((2, width, tall), jnp.float32),
+            pltpu.SemaphoreType.DMA((5,)),
         ],
-        compiler_params=pltpu.CompilerParams(vmem_limit_bytes=56 * 1024 * 1024),
+        compiler_params=pltpu.CompilerParams(
+            vmem_limit_bytes=56 * 1024 * 1024, collective_id=0, has_side_effects=True
+        ),
         name="slice_kernel",
     )(
         motion,
@@ -567,16 +569,7 @@
         encode_table,
         decode_table,
     )
-    other = pl.pallas_call(
-        partner_kernel,
-        out_shape=jax.ShapeDtypeStruct(own.shape, own.dtype),
-        in_specs=[vmem],
-        out_specs=vmem,
-        scratch_shapes=[pltpu.SemaphoreType.DMA, pltpu.SemaphoreType.DMA],
-        compiler_params=pltpu.CompilerParams(collective_id=0, has_side_effects=True),
-        name="partner_kernel",
-    )(own)
-    return jnp.transpose(own + other, (2, 0, 1))
+    return jnp.transpose(total, (2, 0, 1))
 
 
 def on_device(image, coil_maps, psf_phase, line_mask, motion):

time: 36.4 us -> 34.4 us (0.945)
  other arithmetic: 1.91 us -> 0 us
  Pallas kernels: 34.3 us -> 32.4 us
  local copies, waits for them, and re-layouts: 0 us -> 1.77 us
    pallas_call x1 -> x0, Pallas kernels: 3.79 us -> none  [whole_slice(): pl.pallas_call(partner_kernel, out_shape=jax.ShapeDtypeStruct(own.shape,...]
    pallas_call x1, Pallas kernels: 30.5 us -> 32.4 us  [whole_slice(): pl.pallas_call(slice_kernel, out_shape=jax.ShapeDtypeStruct((2, width, he...]
    transpose x1 -> x0, other arithmetic: 1.91 us -> none  [whole_slice(): return jnp.transpose(own + other, (2, 0, 1))]
    unnamed x0 -> x1, local copies, waits for them, and re-layouts: none -> 1.77 us
where the time goes in v2:
time: 34.4 us; the launch traced here: 34.2 us
  Pallas kernels  32.4 us (94%)
  local copies, waits for them, and re-layouts  1.77 us (5%)
    pallas_call x1, Pallas kernels, whole_slice(): pl.pallas_call(slice_kernel, out_shape=jax.ShapeDtypeStruct((2, width, he...  32.4 us
    unnamed x1, local copies, waits for them, and re-layouts  1.77 us

profile of v2, /device:TPU:7, one launch (start us, length us, event | category | flops | bytes accessed | tf_op | source)
XLA Modules:
  0.0 34.2 jit_solution(2277806432569306486)
XLA Ops:
  0.0 32.4 %slice_kernel.1 = f32[2,192,200]{2,1,0:T(8,128)} custom-call(s32[1,3]{1,0:T(1,128)} %motion_ref.1, s32[1,200]{1,0:T(1,128)} %mask_ref.1, f32[2,192,200]{2,1,0:T(8,128)} %bitcast.5, f32[200,576]{1,0:T(8,128)} %psf_ref.1, bf16[2,384,192]{2,1,0:T(8,128)(2,1)} %constant.10.clone.row_ref, bf16[2,256,512]{2,1,0:T(8,128)(2,1)} %constant.11.clone.column_ref, ...), custom_call_target="tpu_custom_call" | custom-call | tf_op jit(solution)/shard_map/slice_kernel/pallas_call | solution.py:534
  32.5 1.8 %copy.11 = f32[200,2,192]{0,2,1:T(8,128)} copy(f32[200,2,192]{0,2,1:T(8,128)} %bitcast.4) | data formatting | bytes 614400
